TPU v7x, 32 devices: a whole 2x2x4 slice. The times are simulated.
32 devices in a mesh: emb: 4 (over x, core), seq: 8 (over z, y).
Axes of the slice: x: 2, y: 2, z: 4, core: 2. Of those that a mesh axis runs over, the one named last changes fastest.
Arguments:
- token_rows: int32 [4, 4096], P('emb', 'seq'), may hold values from 0 to 4223, as said below
- segment_ids: int32 [4, 4096], P('emb', 'seq'), may hold values from 0 to 3, never falling along the last dimension, each value on 1 to 2048 neighbouring positions
- requests: int32 [32, 32, 4], P(('emb', 'seq')), may hold values from 0 to 8191, as said below
- hot_table: bfloat16 [4096, 512], replicated, may hold values from -6 to 6
- cold_table: bfloat16 [262144, 512], P(('emb', 'seq')), may hold values from -6 to 6
- input_weight: bfloat16 [512, 2048], replicated, may hold values from -0.75 to 0.75
- output_weight: bfloat16 [512, 512], replicated, may hold values from -0.25 to 0.25
- up_weight: bfloat16 [512, 2048], replicated, may hold values from -0.25 to 0.25
- down_weight: bfloat16 [2048, 512], replicated, may hold values from -0.125 to 0.125
Outputs:
- layer_output: bfloat16 [4, 4096, 512], P('emb', 'seq')
Inputs may be any that keep to these rules, and one draw needn't show every extreme that they name: `token_rows`: A value below 4096 names that row of hot_table. A value 4096 + o * 4 + k names slot k of the holding device's requests to owner o, and that slot is always a live one. Exactly 256 positions of each device name request slots. For each requesting device and owner the live requests fill slots 0 to c - 1, with c from 1 to 4; dead slots hold 0. Some owners, the same ones for all requesters, get all 4 slots live from every device, and every draw has at least one such owner. `segment_ids`: segment numbers never fall along a sequence.
All inputs are finite; a program needn't handle non-finite values.
Results may differ from a plain program's by a relative error of at most 0.0087.
Values may be sent and summed in bfloat16 or wider, within the bound.
No kernel may reach another device: no remote copies, remote signals or barrier semaphores. Data moves between devices by JAX's collectives and lax.ppermute only.
A program may use at most 128 MiB of HBM per device.

v0:
```python
import functools
import math

import jax
import jax.numpy as jnp
from jax import lax
from jax.experimental import pallas as pl
from jax.experimental.pallas import tpu as pltpu
from jax.sharding import PartitionSpec as P

H = 16
LANES = 128
PICK = 8
SEGMENTS = 4
epsilon = 1e-06
APART = 2.0**30
f32 = jnp.float32
bf16 = jnp.bfloat16

VMEM = pl.BlockSpec(memory_space=pltpu.VMEM)
SMEM = pl.BlockSpec(memory_space=pltpu.SMEM)
HBM = pl.BlockSpec(memory_space=pl.ANY)


def call(body, out_shape, in_specs, out_specs, scratch=(), flops=0, name=None, size=60):
    return pl.pallas_call(
        body,
        out_shape=out_shape,
        in_specs=in_specs,
        out_specs=out_specs,
        scratch_shapes=list(scratch),
        compiler_params=pltpu.CompilerParams(vmem_limit_bytes=size * 1024 * 1024),
        cost_estimate=pl.CostEstimate(flops=flops, bytes_accessed=0, transcendentals=0),
        name=name,
    )


def dot(a, b, ca, cb):
    return lax.dot_general(a, b, (((ca,), (cb,)), ((), ())), preferred_element_type=f32)


def silu(x):
    half = x * 0.5
    return half * jnp.tanh(half) + half


def rms(x, axis):
    return lax.rsqrt(jnp.mean(x * x, axis=axis, keepdims=True) + epsilon)


def owner_body(
    head_groups, emb, seq, cap, message_hbm, message, cold, weight_hbm, after,
    sent, tiles, weight, req, sem, weight_sem,
):
    count = emb * seq * cap
    per = LANES // cap
    span = seq * cap
    split = weight.shape[0] // LANES
    raw = cap * split
    load = pltpu.make_async_copy(weight_hbm, weight, weight_sem)

    asked = pltpu.make_async_copy(message_hbm.at[:, message.shape[1] - 2, :], req, weight_sem)
    asked.start()
    asked.wait()
    batch = 8

    def fetch(j, _):
        for i in range(batch):
            for k in range(cap):
                row = req[j * batch + i, k]
                base = pl.multiple_of((row // PICK) * PICK, PICK)
                slot = pl.multiple_of(((j * batch + i) * cap + k) * PICK, PICK)
                pltpu.make_async_copy(
                    cold.at[pl.ds(base, PICK)], tiles.at[pl.ds(slot, PICK)], sem
                ).start()
        return 0

    lax.fori_loop(0, emb * seq // batch, fetch, 0)
    load.start()
    tags = message[:, message.shape[1] - 2, :]
    picks = []
    for group in range(count // LANES):
        owner = lax.broadcasted_iota(jnp.int32, (per, LANES), 0)
        lane = lax.broadcasted_iota(jnp.int32, (per, LANES), 1)
        mine = jnp.where(lane // cap == owner, tags[group * per : (group + 1) * per], 0)
        wanted = jnp.sum(mine, axis=0, keepdims=True)
        place = lax.broadcasted_iota(jnp.int32, (LANES * PICK, LANES), 0)
        column = lax.broadcasted_iota(jnp.int32, (1, LANES), 1)
        pick = (place == column * PICK + wanted % PICK).astype(f32)
        picks.append(pick.T.astype(bf16))
    line = lax.broadcasted_iota(jnp.int32, (per * raw, LANES), 0)
    source = lax.broadcasted_iota(jnp.int32, (per * raw, LANES), 1)
    repeat = ((line // raw) * cap + line % cap == source).astype(f32).astype(bf16)
    chunk = (lax.broadcasted_iota(jnp.int32, (per * raw, LANES), 0) % raw) // cap
    pltpu.make_async_copy(cold.at[pl.ds(0, count * PICK)], tiles, sem).wait()
    load.wait()
    for group in range(count // LANES):
        block = tiles[group * LANES * PICK : (group + 1) * LANES * PICK]
        part = dot(picks[group], block, 1, 0)
        normed = (part * rms(part, 1)).astype(bf16)
        projected = dot(normed, weight[...], 1, 0).astype(bf16)
        spread = dot(repeat, part.astype(bf16), 1, 0)
        lines = spread[:, :LANES]
        for c in range(1, split):
            lines = jnp.where(chunk == c, spread[:, c * LANES : (c + 1) * LANES], lines)
        kept = sent.shape[1] - raw
        sent[group * per : (group + 1) * per, kept:] = lines.astype(bf16).reshape(
            per, raw, LANES
        )
        for local in range(LANES // span):
            member = group * (LANES // span) + local
            for g in range(seq):
                piece = projected[local * span : (local + 1) * span]
                if head_groups == 1:
                    sent[member * seq + g, :span] = piece[:, g * LANES : (g + 1) * LANES]
                else:
                    low = piece[:, (2 * g) * LANES : (2 * g + 1) * LANES]
                    high = piece[:, (2 * g + 1) * LANES : (2 * g + 2) * LANES]
                    sent[member * seq + g, :span] = jnp.concatenate(
                        [high[:, 32:64], low[:, 32:]], axis=1
                    )
                    sent[member * seq + g, span:kept] = jnp.concatenate(
                        [high[span // 2 :, 64:], high[: span // 2, 64:]], axis=1
                    )


def message_body(ids, segments, wanted, out):
    devices, lines, _ = out.shape
    cap = wanted.shape[0]
    lane = lax.broadcasted_iota(jnp.int32, (1, LANES), 1)
    edges = jnp.zeros((1, LANES), jnp.int32)
    for s in range(1, SEGMENTS):
        below = jnp.sum((segments[...] < s).astype(jnp.int32), axis=1, keepdims=True)
        edges = jnp.where(lane == s, below, edges)
    for j in range(lines - 2):
        out[:, j, :] = jnp.broadcast_to(
            ids[:, j * LANES : (j + 1) * LANES], (devices, LANES)
        )
    asked = wanted[...].astype(f32).T.astype(jnp.int32)
    tags = jnp.broadcast_to(asked[:, 0:1], (devices, LANES))
    for k in range(1, cap):
        tags = jnp.where(lane % cap == k, asked[:, k : k + 1], tags)
    out[:, lines - 2, :] = tags
    out[:, lines - 1, :] = jnp.broadcast_to(edges, (devices, LANES))


def hot_body(head_groups, step, own, after, weight_hbm, table_hbm, out_hbm, weight, table, out, sems):
    hot = table.shape[0]
    chunks = hot // step
    lanes = weight.shape[1]
    begin = pl.multiple_of(own[0] * lanes, lanes)
    first = pltpu.make_async_copy(
        weight_hbm.at[:, pl.ds(begin, lanes)], weight, sems.at[2 * chunks]
    )
    first.start()
    loads = [
        pltpu.make_async_copy(
            table_hbm.at[pl.ds(c * step, step)], table.at[pl.ds(c * step, step)], sems.at[c]
        )
        for c in range(chunks)
    ]
    saves = [
        pltpu.make_async_copy(
            out.at[:, pl.ds(c * step, step)],
            out_hbm.at[:, pl.ds(c * step, step)],
            sems.at[chunks + c],
        )
        for c in range(chunks)
    ]
    for load in loads:
        load.start()
    first.wait()
    wide = weight[...].astype(f32).T.astype(bf16)
    for c in range(chunks):
        at = slice(c * step, (c + 1) * step)
        loads[c].wait()
        x = table[at].astype(f32)
        normed = (x * rms(x, 1)).astype(bf16)
        flat = dot(wide, normed, 1, 1).astype(bf16)
        if head_groups == 1:
            out[:, at] = flat
        else:
            out[0:32, at] = flat[160:192]
            out[32:128, at] = flat[32:128]
            out[128:192, at] = flat[192:256]
        saves[c].start()
    for save in saves:
        save.wait()


def item_row(heard, at, lines):
    return jnp.concatenate([heard[at, j : j + 1, :] for j in range(lines)], axis=1)


def spread_body(step, seq, lines, member, heard, table_hbm, out_hbm, base, table, out, sems):
    tokens = lines * LANES
    hot = table.shape[1]
    load = pltpu.make_async_copy(table_hbm, table, sems.at[seq])
    load.start()
    base[...] = lax.broadcasted_iota(jnp.int32, base.shape, 0).astype(jnp.int16)
    load.wait()

    def save(s):
        column = pl.multiple_of(s * tokens, tokens)
        return pltpu.make_async_copy(
            out.at[:, pl.ds(column, tokens)], out_hbm.at[:, pl.ds(column, tokens)], sems.at[s]
        )

    def one(s, _):
        own = item_row(heard, member[0] * seq + s, lines)
        column = pl.multiple_of(s * tokens, tokens)
        acc = jnp.zeros((out.shape[0], tokens), f32)
        for c in range(hot // step):
            place = (own - c * step).astype(jnp.int16)
            pick = jnp.where(base[...] == place, jnp.ones((), bf16), jnp.zeros((), bf16))
            acc = acc + dot(table[:, c * step : (c + 1) * step], pick, 1, 0)
        out[:, pl.ds(column, tokens)] = acc.astype(bf16)
        save(s).start()
        return 0

    lax.fori_loop(0, seq, one, 0)
    for s in range(seq):
        save(s).wait()


def own_body(
    hot, cap, step, ids, got, table_hbm, weight_hbm, embedded_hbm, gates_hbm,
    table, weight, embedded, gates, sems,
):
    tokens, model = embedded.shape
    chunks = hot // step
    loads = [
        pltpu.make_async_copy(
            table_hbm.at[pl.ds(c * step, step)], table.at[pl.ds(c * step, step)], sems.at[3 + c]
        )
        for c in range(chunks)
    ]
    for load in loads:
        load.start()
    load = pltpu.make_async_copy(weight_hbm, weight, sems.at[0])
    load.start()
    items = jnp.broadcast_to(ids[...].astype(f32), (8, tokens)).T[:, 0:1].astype(jnp.int32)
    split = model // LANES
    raw = cap * split
    owners = got.shape[0]
    lines = got[:, got.shape[1] - raw :, :].reshape(owners * raw, LANES)
    slot = items - hot
    code = jnp.where(slot >= 0, (slot // cap) * raw + slot % cap, -raw)
    place = lax.broadcasted_iota(jnp.int32, (tokens, owners * raw), 1)
    parts = []
    for c in range(split):
        pick = (place == code + c * cap).astype(f32).astype(bf16)
        parts.append(dot(pick, lines, 1, 0))
    emb = jnp.concatenate(parts, axis=1)
    for c in range(chunks):
        loads[c].wait()
        place = lax.broadcasted_iota(jnp.int32, (tokens, step), 1) + c * step
        pick = (place == items).astype(f32).astype(bf16)
        emb = emb + dot(pick, table[c * step : (c + 1) * step], 1, 0)
    embedded[...] = emb.astype(bf16)
    save = pltpu.make_async_copy(embedded, embedded_hbm, sems.at[1])
    save.start()
    normed = (emb * rms(emb, 1)).astype(bf16)
    load.wait()
    step = weight.shape[1] // H
    width = model // H
    wide = jnp.concatenate(
        [
            weight[:, h * step : (h + 1) * step].astype(f32).T[:width]
            for h in range(H)
        ],
        axis=0,
    ).astype(bf16)
    u = dot(wide, normed, 1, 1).astype(bf16).astype(f32)
    gates[...] = silu(u)
    other = pltpu.make_async_copy(gates, gates_hbm, sems.at[2])
    other.start()
    save.wait()
    other.wait()


def attend_body(
    head_groups, seq, cap, hot, width, bq, bk, lines, member, heard, table_hbm, got, out,
    qt, vt, kr, score0, score1, weight0, weight1, total, table, base, sems
):
    tokens = lines * LANES
    length = seq * tokens
    owners = got.shape[0]
    quarter = 16 // cap
    span = seq * cap
    depth = qt.shape[1]
    kept = span if head_groups == 1 else span + span // 2
    loads = [
        pltpu.make_async_copy(
            table_hbm.at[:, pl.ds(s * tokens, tokens)],
            table.at[:, pl.ds(s * tokens, tokens)],
            sems.at[s],
        )
        for s in range(seq)
    ]
    for load in loads:
        load.start()
    mine = heard[pl.ds(member[0] * seq, seq), lines + 1, :]
    lane = lax.broadcasted_iota(jnp.int32, mine.shape, 1)
    edges = [jnp.sum(jnp.where(lane == i, mine, 0)) for i in range(1, SEGMENTS)]
    base[...] = lax.broadcasted_iota(jnp.int32, base.shape, 0).astype(jnp.int16)
    for part in range(span // 16):
        a = got[:, part * 16 : (part + 1) * 16, :].reshape(owners * 16, LANES)
        if head_groups == 1:
            lhs = a.astype(f32).T.astype(bf16)
        else:
            b = got[:, span:kept, :].reshape(owners * 16, LANES).astype(f32).T
            b = b[64:] if part == 0 else b[:64]
            lhs = jnp.concatenate([a.astype(f32).T, b], axis=0).astype(bf16)
        for within in range(quarter):
            s = part * quarter + within
            slot = item_row(heard, member[0] * seq + s, lines) - hot
            code = jnp.where(slot >= 0, (slot // cap) * 16 + within * cap + slot % cap, -1)
            pick = jnp.where(
                base[...] == code.astype(jnp.int16), jnp.ones((), bf16), jnp.zeros((), bf16)
            )
            at = slice(s * tokens, (s + 1) * tokens)
            loads[s].wait()
            full = dot(lhs, pick, 1, 0) + table[:, at].astype(f32)
            full_b = full.astype(bf16)
            spot = s * tokens + lax.broadcasted_iota(jnp.int32, (1, tokens), 1)
            segment = jnp.zeros((1, tokens), jnp.int32)
            for edge in edges:
                segment = segment + (spot >= edge).astype(jnp.int32)
            level = lax.broadcasted_iota(jnp.int32, (depth - width, tokens), 0)
            same = (level == segment).astype(f32)
            if head_groups == 1:
                order = ((32, 64, 96),)
            else:
                order = ((32, 64, 96), (0, 128, 160))
            for h, (v, q, k) in enumerate(order):
                vt[h, :, at] = full_b[v : v + width]
                qt[h, :, at] = jnp.concatenate(
                    [full_b[q : q + width], ((same - 1.0) * APART).astype(bf16)], axis=0
                )
                kr[h, at, :] = jnp.concatenate([full[k : k + width], same], axis=0).T.astype(
                    bf16
                )
    scale = 0.5 / math.sqrt(width)
    blocks = length // bq

    def low(qb):
        best = 0
        for edge in edges:
            best = jnp.where(qb * bq >= edge, edge, best)
        return best // bk

    def high(qb):
        return (qb + 1) * (bq // bk) - 1

    def count(qb, n):
        return n + high(qb) - low(qb) + 1

    tiles = lax.fori_loop(0, blocks, count, 0)

    ahead = lax.broadcasted_iota(jnp.int32, (bk, bq), 0) - lax.broadcasted_iota(
        jnp.int32, (bk, bq), 1
    )
    score = (score0, score1)
    weights = (weight0, weight1)

    def half_step(i, slot, now, then, past):
        qb, kb = then
        keep = ahead <= qb * bq - kb * bk
        for h in range(head_groups):
            half = score[1 - slot][h] * scale
            weight = half * jnp.tanh(half) + half
            weights[1 - slot][h] = jnp.where(keep, weight, 0.0).astype(bf16)
        qb, kb = past
        q0 = pl.multiple_of(qb * bq, bq)
        k0 = pl.multiple_of(kb * bk, bk)
        device = q0 // tokens
        column = pl.multiple_of(q0 % tokens, bq)
        fresh = kb == low(qb)
        live = (i >= 2) & (i < tiles + 2)
        for h in range(head_groups):
            part = dot(vt[h, :, pl.ds(k0, bk)], weights[slot][h], 1, 0)
            part = jnp.where(live, part + jnp.where(fresh, 0.0, total[h]), total[h])
            total[h] = part
            out[device, h * width : (h + 1) * width, pl.ds(column, bq)] = part.astype(bf16)
        qb, kb = now
        q0 = pl.multiple_of(qb * bq, bq)
        k0 = pl.multiple_of(kb * bk, bk)
        for h in range(head_groups):
            score[slot][h] = dot(kr[h, pl.ds(k0, bk), :], qt[h, :, pl.ds(q0, bq)], 1, 0)
        done = kb == high(qb)
        last = done & (qb == blocks - 1)
        next_q = jnp.where(done & ~last, qb + 1, qb)
        next_k = jnp.where(last, kb, jnp.where(done, low(next_q), kb + 1))
        return next_q, next_k

    def step(j, state):
        now, then, past = state
        after = half_step(2 * j, 0, now, then, past)
        later = half_step(2 * j + 1, 1, after, now, then)
        return later, after, now

    start = (jnp.int32(0), jnp.int32(0))
    for ref in (score1, weight0):
        ref[...] = jnp.zeros(ref.shape, ref.dtype)
    total[...] = jnp.zeros(total.shape, f32)
    lax.fori_loop(0, (tiles + 3) // 2, step, (start, start, start))


def final_body(
    returned, gates_hbm, embedded_hbm, out_hbm, up_hbm, down_hbm, result,
    gates, embedded, out_weight, up, down, out, sems,
):
    tokens = out.shape[0]
    pairs = (
        (gates_hbm, gates),
        (out_hbm, out_weight),
        (embedded_hbm, embedded),
        (up_hbm, up),
        (down_hbm, down),
    )
    loads = [
        pltpu.make_async_copy(there, here, sems.at[i]) for i, (there, here) in enumerate(pairs)
    ]
    for load in loads:
        load.start()
    att = returned[...].astype(f32)
    att = att * rms(att, 0)
    loads[0].wait()
    heads = (att * gates[...]).astype(bf16)
    loads[1].wait()
    mixed = dot(heads, out_weight[...], 0, 0)
    loads[2].wait()
    hidden = embedded[...].astype(f32) + mixed
    normed = (hidden * rms(hidden, 1)).astype(bf16)
    loads[3].wait()
    saves = []
    half = tokens // 2
    for part in range(2):
        at = slice(part * half, (part + 1) * half)
        active = silu(dot(normed[at], up[...], 1, 0)).astype(bf16)
        if part == 0:
            loads[4].wait()
        out[at] = (hidden[at] + dot(active, down[...], 1, 0)).astype(bf16)
        saves.append(
            pltpu.make_async_copy(
                out.at[pl.ds(part * half, half)],
                result.at[pl.ds(part * half, half)],
                sems.at[5 + part],
            )
        )
        saves[-1].start()
    for save in saves:
        save.wait()


def local(
    token_rows,
    segment_ids,
    requests,
    hot_table,
    cold_table,
    input_weight,
    output_weight,
    up_weight,
    down_weight,
):
    both = ("emb", "seq")
    emb = lax.axis_size("emb")
    seq = lax.axis_size("seq")
    devices = emb * seq
    cap = requests.shape[2]
    hot, model = hot_table.shape
    tokens = token_rows.shape[1]
    groups = H // seq
    width = model // H
    own = lax.axis_index("seq")
    member = lax.axis_index("emb")
    span = seq * cap

    lines = tokens // LANES
    raw = cap * model // LANES
    message = call(
        message_body,
        jax.ShapeDtypeStruct((devices, lines + 2, LANES), jnp.int32),
        [VMEM] * 3,
        VMEM,
        name="message",
        size=60,
    )(token_rows, segment_ids, requests[0].T)
    heard = lax.all_to_all(message, both, split_axis=0, concat_axis=0, tiled=True)

    kept = LANES if groups == 1 else 192
    step = 512
    hot_projected = call(
        functools.partial(hot_body, groups, step),
        jax.ShapeDtypeStruct((kept, hot), bf16),
        [SMEM, HBM, HBM, HBM],
        HBM,
        [
            pltpu.VMEM((model, groups * 4 * width), bf16),
            pltpu.VMEM((hot, model), bf16),
            pltpu.VMEM((kept, hot), bf16),
            pltpu.SemaphoreType.DMA((2 * (hot // step) + 1,)),
        ],
        flops=2 * hot * model * 256,
        name="hot",
        size=60,
    )(own.astype(jnp.int32).reshape(1), message, input_weight, hot_table)

    span_lines = span if groups == 1 else span + span // 2
    sent = call(
        functools.partial(owner_body, groups, emb, seq, cap),
        jax.ShapeDtypeStruct((devices, span_lines + raw, LANES), bf16),
        [HBM, VMEM, HBM, HBM, HBM],
        VMEM,
        [
            pltpu.VMEM((devices * cap * PICK, model), bf16),
            pltpu.VMEM(input_weight.shape, bf16),
            pltpu.SMEM((devices, LANES), jnp.int32),
            pltpu.SemaphoreType.DMA,
            pltpu.SemaphoreType.DMA,
        ],
        flops=2 * devices * cap * model * 2048,
        name="owner",
        size=60,
    )(heard, heard, cold_table, input_weight, hot_projected)
    got = lax.all_to_all(sent, both, split_axis=0, concat_axis=0, tiled=True)

    place = member.astype(jnp.int32).reshape(1)
    spread = call(
        functools.partial(spread_body, step, seq, lines),
        jax.ShapeDtypeStruct((kept, seq * tokens), bf16),
        [SMEM, VMEM, HBM],
        HBM,
        [
            pltpu.VMEM((step, tokens), jnp.int16),
            pltpu.VMEM((kept, hot), bf16),
            pltpu.VMEM((kept, seq * tokens), bf16),
            pltpu.SemaphoreType.DMA((seq + 1,)),
        ],
        flops=2 * seq * tokens * hot * 256,
        name="spread",
        size=60,
    )(place, heard, hot_projected)

    deep = width + 16
    tile = (groups, BK, BQ)
    attended = call(
        functools.partial(attend_body, groups, seq, cap, hot, width, BQ, BK, lines),
        jax.ShapeDtypeStruct((seq, groups * width, tokens), bf16),
        [SMEM, VMEM, HBM, VMEM],
        VMEM,
        [
            pltpu.VMEM((groups, deep, seq * tokens), bf16),
            pltpu.VMEM((groups, width, seq * tokens), bf16),
            pltpu.VMEM((groups, seq * tokens, deep), bf16),
            pltpu.VMEM(tile, f32),
            pltpu.VMEM(tile, f32),
            pltpu.VMEM(tile, bf16),
            pltpu.VMEM(tile, bf16),
            pltpu.VMEM((groups, width, BQ), f32),
            pltpu.VMEM((kept, seq * tokens), bf16),
            pltpu.VMEM((devices * 16, tokens), jnp.int16),
            pltpu.SemaphoreType.DMA((seq,)),
        ],
        flops=10**10,
        name="attend",
        size=60,
    )(place, heard, spread, got)
    returned = lax.all_to_all(attended, "seq", split_axis=0, concat_axis=0, tiled=True)

    embedded, gates = call(
        functools.partial(own_body, hot, cap, step),
        (
            jax.ShapeDtypeStruct((tokens, model), bf16),
            jax.ShapeDtypeStruct((model, tokens), f32),
        ),
        [VMEM, VMEM, HBM, HBM],
        (HBM, HBM),
        [
            pltpu.VMEM((hot, model), bf16),
            pltpu.VMEM(input_weight.shape, bf16),
            pltpu.VMEM((tokens, model), bf16),
            pltpu.VMEM((model, tokens), f32),
            pltpu.SemaphoreType.DMA((3 + hot // step,)),
        ],
        flops=2 * tokens * model * model,
        name="own",
        size=60,
    )(token_rows, got, hot_table, input_weight)
    result = call(
        final_body,
        jax.ShapeDtypeStruct((tokens, model), bf16),
        [VMEM, HBM, HBM, HBM, HBM, HBM],
        HBM,
        [
            pltpu.VMEM((model, tokens), f32),
            pltpu.VMEM((tokens, model), bf16),
            pltpu.VMEM(output_weight.shape, bf16),
            pltpu.VMEM(up_weight.shape, bf16),
            pltpu.VMEM(down_weight.shape, bf16),
            pltpu.VMEM((tokens, model), bf16),
            pltpu.SemaphoreType.DMA((7,)),
        ],
        flops=2 * tokens * model * 4096,
        name="final",
        size=60,
    )(returned.reshape(model, tokens), gates, embedded, output_weight, up_weight, down_weight)
    return result[None]


BQ = 256
BK = 256


def solution(mesh):
    placed = (
        P("emb", "seq"),
        P("emb", "seq"),
        P(("emb", "seq"), None, None),
        P(),
        P(("emb", "seq"), None),
        P(),
        P(),
        P(),
        P(),
    )
    return jax.shard_map(
        local, mesh=mesh, in_specs=placed, out_specs=P("emb", "seq", None), check_vma=False
    )
```

profile of v0, /device:TPU:0, one launch (start us, length us, event | category | flops | bytes accessed | tf_op | source)
XLA Modules:
  0.0 89.2 jit_solution(8588131997773365551)
XLA Ops:
  0.0 1.6 %message.1.after = s32[32,6,128]{2,1,0:T(8,128)} custom-call(s32[1,512]{1,0:T(1,128)} %ids.3, s32[1,512]{1,0:T(1,128)} %segments.1, s32[4,32]{1,0:T(4,128)} %bitcast.8), custom_call_target="tpu_custom_call" | custom-call | tf_op jit(solution)/shard_map/message/pallas_call | solution.py:483
  1.6 7.3 %all-to-all-start = ((s32[32,6,128]{2,1,0:T(8,128)}), s32[32,6,128]{2,1,0:T(8,128)S(1)}, u32[]{:S(2)}, u32[]{:S(2)}) async-start(s32[32,6,128]{2,1,0:T(8,128)} %message.1.after), calls=%async_computation | async-start | bytes 262144 | tf_op jit(solution)/shard_map/all_to_all | solution.py:491
  8.9 5.6 %hot.1.table_hbm.after = bf16[192,4096]{1,0:T(8,128)(2,1)} custom-call(s32[1]{0:T(128)} %bitcast.3.own, s32[32,6,128]{2,1,0:T(8,128)} %message.1.after, bf16[512,2048]{1,0:T(8,128)(2,1)} %weight_hbm.5, bf16[4096,512]{1,0:T(8,128)(2,1)} %table_hbm.3), custom_call_target="tpu_custom_call" | custom-call | flops 1073741824 | tf_op jit(solution)/shard_map/hot/pallas_call | solution.py:495
  14.6 2.1 %all-to-all-done.heard.message_hbm.message = s32[32,6,128]{2,1,0:T(8,128)S(1)} async-done(((s32[32,6,128]{2,1,0:T(8,128)}), s32[32,6,128]{2,1,0:T(8,128)S(1)}, u32[]{:S(2)}, u32[]{:S(2)}) %all-to-all-start) | async-done | bytes 98336 | tf_op jit(solution)/shard_map/all_to_all | solution.py:491
  16.7 0.0 copy-start.1
  16.7 0.6 copy-done.1
  17.4 6.3 %owner.1 = bf16[32,64,128]{2,1,0:T(8,128)(2,1)} custom-call(s32[32,6,128]{2,1,0:T(8,128)} %copy-done.1, s32[32,6,128]{2,1,0:T(8,128)} %copy-done.1, bf16[8192,512]{1,0:T(8,128)(2,1)} %cold.1, bf16[512,2048]{1,0:T(8,128)(2,1)} %weight_hbm.5, bf16[192,4096]{1,0:T(8,128)(2,1)} %hot.1.table_hbm.after), custom_call_target="tpu_custom_call" | custom-call | flops 268435456 | tf_op jit(solution)/shard_map/owner/pallas_call | solution.py:512
  23.6 5.3 %all-to-all-start.1 = ((bf16[32,64,128]{2,1,0:T(8,128)(2,1)}), bf16[32,64,128]{2,1,0:T(8,128)(2,1)S(1)}, u32[]{:S(2)}, u32[]{:S(2)}) async-start(bf16[32,64,128]{2,1,0:T(8,128)(2,1)} %owner.1), calls=%async_computation.1 | async-start | bytes 1048576 | tf_op jit(solution)/shard_map/all_to_all | solution.py:528
  29.0 11.1 %spread.1.table_hbm = bf16[192,4096]{1,0:T(8,128)(2,1)} custom-call(s32[1]{0:T(128)} %bitcast.member, s32[32,6,128]{2,1,0:T(8,128)} %copy-done.1, bf16[192,4096]{1,0:T(8,128)(2,1)} %hot.1.table_hbm.after), custom_call_target="tpu_custom_call" | custom-call | flops 8589934592 | tf_op jit(solution)/shard_map/spread/pallas_call | solution.py:531
  40.1 5.1 %all-to-all-done.1.got = bf16[32,64,128]{2,1,0:T(8,128)(2,1)S(1)} async-done(((bf16[32,64,128]{2,1,0:T(8,128)(2,1)}), bf16[32,64,128]{2,1,0:T(8,128)(2,1)S(1)}, u32[]{:S(2)}, u32[]{:S(2)}) %all-to-all-start.1) | async-done | bytes 524320 | tf_op jit(solution)/shard_map/all_to_all | solution.py:528
  45.2 0.0 copy-start
  45.2 0.8 copy-done
  46.0 19.5 %attend.1 = bf16[8,64,512]{2,1,0:T(8,128)(2,1)} custom-call(s32[1]{0:T(128)} %bitcast.member, s32[32,6,128]{2,1,0:T(8,128)} %copy-done.1, bf16[192,4096]{1,0:T(8,128)(2,1)} %spread.1.table_hbm, bf16[32,64,128]{2,1,0:T(8,128)(2,1)} %copy-done), custom_call_target="tpu_custom_call" | custom-call | flops 10000000000 | tf_op jit(solution)/shard_map/attend/pallas_call | solution.py:549
  65.5 3.7 %all-to-all-start.2 = ((bf16[8,64,512]{2,1,0:T(8,128)(2,1)}), bf16[8,64,512]{2,1,0:T(8,128)(2,1)S(1)}, u32[]{:S(2)}, u32[]{:S(2)}) async-start(bf16[8,64,512]{2,1,0:T(8,128)(2,1)} %attend.1), calls=%async_computation.2 | async-start | bytes 1048576 | tf_op jit(solution)/shard_map/all_to_all | solution.py:571
  69.2 7.9 %own.1 = (bf16[512,512]{1,0:T(8,128)(2,1)}, f32[512,512]{1,0:T(8,128)}) custom-call(s32[1,512]{1,0:T(1,128)} %ids.3, bf16[32,64,128]{2,1,0:T(8,128)(2,1)} %copy-done, bf16[4096,512]{1,0:T(8,128)(2,1)} %table_hbm.3, bf16[512,2048]{1,0:T(8,128)(2,1)} %weight_hbm.5), custom_call_target="tpu_custom_call" | custom-call | flops 268435456 | tf_op jit(solution)/shard_map/own/pallas_call | solution.py:573
  77.1 4.3 %all-to-all-done.2 = bf16[8,64,512]{2,1,0:T(8,128)(2,1)S(1)} async-done(((bf16[8,64,512]{2,1,0:T(8,128)(2,1)}), bf16[8,64,512]{2,1,0:T(8,128)(2,1)S(1)}, u32[]{:S(2)}, u32[]{:S(2)}) %all-to-all-start.2) | async-done | bytes 524320 | tf_op jit(solution)/shard_map/all_to_all | solution.py:571
  81.4 0.0 copy-start.2
  81.4 0.8 copy-done.2
  82.2 6.8 %final.1 = bf16[512,512]{1,0:T(8,128)(2,1)} custom-call(bf16[512,512]{1,0:T(8,128)(2,1)} %bitcast.7, f32[512,512]{1,0:T(8,128)} %get-tuple-element.7.gates_hbm, bf16[512,512]{1,0:T(8,128)(2,1)} %get-tuple-element.8.embedded_hbm, bf16[512,512]{1,0:T(8,128)(2,1)} %out_hbm.1, bf16[512,2048]{1,0:T(8,128)(2,1)} %up_hbm.1, bf16[2048,512]{1,0:T(8,128)(2,1)} %down_hbm.1), custom_call_target="tpu_custom_call" | custom-call | flops 2147483648 | tf_op jit(solution)/shard_map/final/pallas_call | solution.py:592
Async XLA Ops:
  1.6 15.1 %all-to-all-start = ((s32[32,6,128]{2,1,0:T(8,128)}), s32[32,6,128]{2,1,0:T(8,128)S(1)}, u32[]{:S(2)}, u32[]{:S(2)}) async-start(s32[32,6,128]{2,1,0:T(8,128)} %message.1.after), calls=%async_computation | async-start | bytes 262144 | tf_op jit(solution)/shard_map/all_to_all | solution.py:491
  16.7 0.7 copy-start.1
  23.6 21.6 %all-to-all-start.1 = ((bf16[32,64,128]{2,1,0:T(8,128)(2,1)}), bf16[32,64,128]{2,1,0:T(8,128)(2,1)S(1)}, u32[]{:S(2)}, u32[]{:S(2)}) async-start(bf16[32,64,128]{2,1,0:T(8,128)(2,1)} %owner.1), calls=%async_computation.1 | async-start | bytes 1048576 | tf_op jit(solution)/shard_map/all_to_all | solution.py:528
  45.2 0.8 copy-start
  65.5 15.9 %all-to-all-start.2 = ((bf16[8,64,512]{2,1,0:T(8,128)(2,1)}), bf16[8,64,512]{2,1,0:T(8,128)(2,1)S(1)}, u32[]{:S(2)}, u32[]{:S(2)}) async-start(bf16[8,64,512]{2,1,0:T(8,128)(2,1)} %attend.1), calls=%async_computation.2 | async-start | bytes 1048576 | tf_op jit(solution)/shard_map/all_to_all | solution.py:571
  81.4 0.8 copy-start.2
where the time goes:
time: 90.9 us; the launch traced here: 89.2 us
  Pallas kernels  58.8 us (65%)
  starting transfers between devices  16.3 us (18%)
  waiting for transfers between devices  11.6 us (13%)
  local copies, waits for them, and re-layouts  2.26 us (2%)
    pallas_call x1, Pallas kernels, local(): call(functools.partial(attend_body, groups, seq, cap, hot, width, BQ, BK,...  19.5 us
    pallas_call x1, Pallas kernels, local(): call(functools.partial(spread_body, step, seq, lines), jax.ShapeDtypeStru...  11.1 us
    pallas_call x1, Pallas kernels, local(): call(functools.partial(own_body, hot, cap, step), (jax.ShapeDtypeStruct((...  7.91 us
    all_to_all x1, starting transfers between devices, local(): lax.all_to_all(message, both, split_axis=0, concat_axis=0, tiled=True)  7.33 us
    pallas_call x1, Pallas kernels, local(): call(final_body, jax.ShapeDtypeStruct((tokens, model), bf16), [VMEM, HBM,...  6.82 us
    pallas_call x1, Pallas kernels, local(): call(functools.partial(owner_body, groups, emb, seq, cap), jax.ShapeDtype...  6.28 us
    pallas_call x1, Pallas kernels, local(): call(functools.partial(hot_body, groups, step), jax.ShapeDtypeStruct((kep...  5.65 us
    all_to_all x1, starting transfers between devices, local(): got = lax.all_to_all(sent, both, split_axis=0, concat_axis=0, tiled=True)  5.33 us
  transfers between devices with their start and end apart: 3, of which 3 were waited for; matrix products, arithmetic and copies ran while one was open for 0% of the time, Pallas kernels for 28%

commit v1 on v0

--- a/solution.py
+++ b/solution.py
@@ -49,8 +49,8 @@
 
 
 def owner_body(
-    head_groups, emb, seq, cap, message_hbm, message, cold, weight_hbm, after,
-    sent, tiles, weight, req, sem, weight_sem,
+    head_groups, emb, seq, cap, message_hbm, cold, weight_hbm, after, sent_hbm,
+    sent, tiles, weight, req, tags, sem, weight_sem, sems,
 ):
     count = emb * seq * cap
     per = LANES // cap
@@ -59,8 +59,12 @@
     raw = cap * split
     load = pltpu.make_async_copy(weight_hbm, weight, weight_sem)
 
-    asked = pltpu.make_async_copy(message_hbm.at[:, message.shape[1] - 2, :], req, weight_sem)
+    wanted_line = message_hbm.shape[1] - 2
+    asked = pltpu.make_async_copy(message_hbm.at[:, wanted_line, :], req, sems.at[0])
     asked.start()
+    again = pltpu.make_async_copy(message_hbm.at[:, wanted_line, :], tags, sems.at[1])
+    again.start()
+    load.start()
     asked.wait()
     batch = 8
 
@@ -76,8 +80,7 @@
         return 0
 
     lax.fori_loop(0, emb * seq // batch, fetch, 0)
-    load.start()
-    tags = message[:, message.shape[1] - 2, :]
+    again.wait()
     picks = []
     for group in range(count // LANES):
         owner = lax.broadcasted_iota(jnp.int32, (per, LANES), 0)
@@ -92,6 +95,7 @@
     source = lax.broadcasted_iota(jnp.int32, (per * raw, LANES), 1)
     repeat = ((line // raw) * cap + line % cap == source).astype(f32).astype(bf16)
     chunk = (lax.broadcasted_iota(jnp.int32, (per * raw, LANES), 0) % raw) // cap
+    saves = []
     pltpu.make_async_copy(cold.at[pl.ds(0, count * PICK)], tiles, sem).wait()
     load.wait()
     for group in range(count // LANES):
@@ -122,6 +126,13 @@
                     sent[member * seq + g, span:kept] = jnp.concatenate(
                         [high[span // 2 :, 64:], high[: span // 2, 64:]], axis=1
                     )
+            at = pl.ds(member * seq, seq)
+            saves.append(
+                pltpu.make_async_copy(sent.at[at], sent_hbm.at[at], sems.at[2 + len(saves)])
+            )
+            saves[-1].start()
+    for save in saves:
+        save.wait()
 
 
 def message_body(ids, segments, wanted, out):
@@ -224,8 +235,8 @@
 
 
 def own_body(
-    hot, cap, step, ids, got, table_hbm, weight_hbm, embedded_hbm, gates_hbm,
-    table, weight, embedded, gates, sems,
+    hot, cap, step, ids, got, table_hbm, weight_hbm, out_hbm, carried,
+    table, weight, embedded, gates, out_weight, sems,
 ):
     tokens, model = embedded.shape
     chunks = hot // step
@@ -239,6 +250,8 @@
         load.start()
     load = pltpu.make_async_copy(weight_hbm, weight, sems.at[0])
     load.start()
+    third = pltpu.make_async_copy(out_hbm, out_weight, sems.at[3 + chunks])
+    third.start()
     items = jnp.broadcast_to(ids[...].astype(f32), (8, tokens)).T[:, 0:1].astype(jnp.int32)
     split = model // LANES
     raw = cap * split
@@ -258,8 +271,13 @@
         pick = (place == items).astype(f32).astype(bf16)
         emb = emb + dot(pick, table[c * step : (c + 1) * step], 1, 0)
     embedded[...] = emb.astype(bf16)
-    save = pltpu.make_async_copy(embedded, embedded_hbm, sems.at[1])
+    save = pltpu.make_async_copy(embedded, carried.at[pl.ds(model, tokens)], sems.at[1])
     save.start()
+    third.wait()
+    third = pltpu.make_async_copy(
+        out_weight, carried.at[pl.ds(model + tokens, model)], sems.at[3 + chunks]
+    )
+    third.start()
     normed = (emb * rms(emb, 1)).astype(bf16)
     load.wait()
     step = weight.shape[1] // H
@@ -272,16 +290,17 @@
         axis=0,
     ).astype(bf16)
     u = dot(wide, normed, 1, 1).astype(bf16).astype(f32)
-    gates[...] = silu(u)
-    other = pltpu.make_async_copy(gates, gates_hbm, sems.at[2])
+    gates[...] = silu(u).astype(bf16)
+    other = pltpu.make_async_copy(gates, carried.at[pl.ds(0, model)], sems.at[2])
     other.start()
     save.wait()
+    third.wait()
     other.wait()
 
 
 def attend_body(
     head_groups, seq, cap, hot, width, bq, bk, lines, member, heard, table_hbm, got, out,
-    qt, vt, kr, score0, score1, weight0, weight1, total, table, base, sems
+    qt, vt, kr, score0, score1, weight0, weight1, total, table, base, factor, sems
 ):
     tokens = lines * LANES
     length = seq * tokens
@@ -321,26 +340,25 @@
             )
             at = slice(s * tokens, (s + 1) * tokens)
             loads[s].wait()
-            full = dot(lhs, pick, 1, 0) + table[:, at].astype(f32)
-            full_b = full.astype(bf16)
+            full = dot(lhs, pick, 1, 0).astype(bf16) + table[:, at]
             spot = s * tokens + lax.broadcasted_iota(jnp.int32, (1, tokens), 1)
             segment = jnp.zeros((1, tokens), jnp.int32)
             for edge in edges:
                 segment = segment + (spot >= edge).astype(jnp.int32)
             level = lax.broadcasted_iota(jnp.int32, (depth - width, tokens), 0)
             same = (level == segment).astype(f32)
+            apart = ((same - 1.0) * APART).astype(bf16)
+            same = same.astype(bf16)
             if head_groups == 1:
                 order = ((32, 64, 96),)
             else:
                 order = ((32, 64, 96), (0, 128, 160))
             for h, (v, q, k) in enumerate(order):
-                vt[h, :, at] = full_b[v : v + width]
+                vt[h, :, at] = full[v : v + width]
                 qt[h, :, at] = jnp.concatenate(
-                    [full_b[q : q + width], ((same - 1.0) * APART).astype(bf16)], axis=0
+                    [full[q : q + width], apart], axis=0
                 )
-                kr[h, at, :] = jnp.concatenate([full[k : k + width], same], axis=0).T.astype(
-                    bf16
-                )
+                kr[h, at, :] = jnp.concatenate([full[k : k + width], same], axis=0).T
     scale = 0.5 / math.sqrt(width)
     blocks = length // bq
 
@@ -361,16 +379,17 @@
     ahead = lax.broadcasted_iota(jnp.int32, (bk, bq), 0) - lax.broadcasted_iota(
         jnp.int32, (bk, bq), 1
     )
+    factor[0] = jnp.full((bk, bq), scale, f32)
+    factor[1] = jnp.where(ahead <= 0, scale, 0.0)
     score = (score0, score1)
     weights = (weight0, weight1)
 
     def half_step(i, slot, now, then, past):
         qb, kb = then
-        keep = ahead <= qb * bq - kb * bk
+        ends = (qb == kb).astype(jnp.int32)
         for h in range(head_groups):
-            half = score[1 - slot][h] * scale
-            weight = half * jnp.tanh(half) + half
-            weights[1 - slot][h] = jnp.where(keep, weight, 0.0).astype(bf16)
+            half = score[1 - slot][h] * factor[ends]
+            weights[1 - slot][h] = (half * jnp.tanh(half) + half).astype(bf16)
         qb, kb = past
         q0 = pl.multiple_of(qb * bq, bq)
         k0 = pl.multiple_of(kb * bk, bk)
@@ -407,48 +426,49 @@
     lax.fori_loop(0, (tiles + 3) // 2, step, (start, start, start))
 
 
-def final_body(
-    returned, gates_hbm, embedded_hbm, out_hbm, up_hbm, down_hbm, result,
-    gates, embedded, out_weight, up, down, out, sems,
-):
-    tokens = out.shape[0]
-    pairs = (
-        (gates_hbm, gates),
-        (out_hbm, out_weight),
-        (embedded_hbm, embedded),
-        (up_hbm, up),
-        (down_hbm, down),
-    )
-    loads = [
-        pltpu.make_async_copy(there, here, sems.at[i]) for i, (there, here) in enumerate(pairs)
+def final_body(step, returned, carried_hbm, up_hbm, down_hbm, result, carried, up, down, out, sems):
+    tokens, model = out.shape
+    chunks = up.shape[1] // step
+    places = (pl.ds(0, model), pl.ds(model + tokens, model), pl.ds(model, tokens))
+    gate_load, out_load, embedded_load = [
+        pltpu.make_async_copy(carried_hbm.at[at], carried.at[at], sems.at[i])
+        for i, at in enumerate(places)
     ]
-    for load in loads:
+    ups = []
+    downs = []
+    for c in range(chunks):
+        at = pl.ds(c * step, step)
+        ups.append(pltpu.make_async_copy(up_hbm.at[:, at], up.at[:, at], sems.at[5 + 2 * c]))
+        downs.append(pltpu.make_async_copy(down_hbm.at[at], down.at[at], sems.at[6 + 2 * c]))
+    for load in (gate_load, out_load, embedded_load):
         load.start()
+    for c in range(chunks):
+        ups[c].start()
+        downs[c].start()
     att = returned[...].astype(f32)
     att = att * rms(att, 0)
-    loads[0].wait()
-    heads = (att * gates[...]).astype(bf16)
-    loads[1].wait()
-    mixed = dot(heads, out_weight[...], 0, 0)
-    loads[2].wait()
-    hidden = embedded[...].astype(f32) + mixed
+    gate_load.wait()
+    heads = (att * carried[:model].astype(f32)).astype(bf16)
+    out_load.wait()
+    mixed = dot(heads, carried[model + tokens :], 0, 0)
+    embedded_load.wait()
+    hidden = carried[model : model + tokens].astype(f32) + mixed
     normed = (hidden * rms(hidden, 1)).astype(bf16)
-    loads[3].wait()
+    total = hidden
+    for c in range(chunks):
+        at = slice(c * step, (c + 1) * step)
+        ups[c].wait()
+        active = silu(dot(normed, up[:, at], 1, 0)).astype(bf16)
+        downs[c].wait()
+        if c + 1 < chunks:
+            total = total + dot(active, down[at], 1, 0)
     saves = []
     half = tokens // 2
     for part in range(2):
-        at = slice(part * half, (part + 1) * half)
-        active = silu(dot(normed[at], up[...], 1, 0)).astype(bf16)
-        if part == 0:
-            loads[4].wait()
-        out[at] = (hidden[at] + dot(active, down[...], 1, 0)).astype(bf16)
-        saves.append(
-            pltpu.make_async_copy(
-                out.at[pl.ds(part * half, half)],
-                result.at[pl.ds(part * half, half)],
-                sems.at[5 + part],
-            )
-        )
+        rows = slice(part * half, (part + 1) * half)
+        out[rows] = (total[rows] + dot(active[rows], down[at], 1, 0)).astype(bf16)
+        place = pl.ds(part * half, half)
+        saves.append(pltpu.make_async_copy(out.at[place], result.at[place], sems.at[3 + part]))
         saves[-1].start()
     for save in saves:
         save.wait()
@@ -512,19 +532,22 @@
     sent = call(
         functools.partial(owner_body, groups, emb, seq, cap),
         jax.ShapeDtypeStruct((devices, span_lines + raw, LANES), bf16),
-        [HBM, VMEM, HBM, HBM, HBM],
-        VMEM,
+        [HBM, HBM, HBM, HBM],
+        HBM,
         [
+            pltpu.VMEM((devices, span_lines + raw, LANES), bf16),
             pltpu.VMEM((devices * cap * PICK, model), bf16),
             pltpu.VMEM(input_weight.shape, bf16),
             pltpu.SMEM((devices, LANES), jnp.int32),
+            pltpu.VMEM((devices, LANES), jnp.int32),
             pltpu.SemaphoreType.DMA,
             pltpu.SemaphoreType.DMA,
+            pltpu.SemaphoreType.DMA((2 + emb,)),
         ],
         flops=2 * devices * cap * model * 2048,
         name="owner",
-        size=60,
-    )(heard, heard, cold_table, input_weight, hot_projected)
+        size=52,
+    )(heard, cold_table, input_weight, hot_projected)
     got = lax.all_to_all(sent, both, split_axis=0, concat_axis=0, tiled=True)
 
     place = member.astype(jnp.int32).reshape(1)
@@ -541,7 +564,7 @@
         ],
         flops=2 * seq * tokens * hot * 256,
         name="spread",
-        size=60,
+        size=51,
     )(place, heard, hot_projected)
 
     deep = width + 16
@@ -562,51 +585,49 @@
             pltpu.VMEM((groups, width, BQ), f32),
             pltpu.VMEM((kept, seq * tokens), bf16),
             pltpu.VMEM((devices * 16, tokens), jnp.int16),
+            pltpu.VMEM((2, BK, BQ), f32),
             pltpu.SemaphoreType.DMA((seq,)),
         ],
         flops=10**10,
         name="attend",
-        size=60,
+        size=51,
     )(place, heard, spread, got)
     returned = lax.all_to_all(attended, "seq", split_axis=0, concat_axis=0, tiled=True)
 
-    embedded, gates = call(
+    carried = call(
         functools.partial(own_body, hot, cap, step),
-        (
-            jax.ShapeDtypeStruct((tokens, model), bf16),
-            jax.ShapeDtypeStruct((model, tokens), f32),
-        ),
-        [VMEM, VMEM, HBM, HBM],
-        (HBM, HBM),
+        jax.ShapeDtypeStruct((2 * model + tokens, model), bf16),
+        [VMEM, VMEM, HBM, HBM, HBM],
+        HBM,
         [
             pltpu.VMEM((hot, model), bf16),
             pltpu.VMEM(input_weight.shape, bf16),
             pltpu.VMEM((tokens, model), bf16),
-            pltpu.VMEM((model, tokens), f32),
-            pltpu.SemaphoreType.DMA((3 + hot // step,)),
+            pltpu.VMEM((model, tokens), bf16),
+            pltpu.VMEM((model, model), bf16),
+            pltpu.SemaphoreType.DMA((4 + hot // step,)),
         ],
         flops=2 * tokens * model * model,
         name="own",
-        size=60,
-    )(token_rows, got, hot_table, input_weight)
+        size=51,
+    )(token_rows, got, hot_table, input_weight, output_weight)
+    hidden_chunks = up_weight.shape[1] // step
     result = call(
-        final_body,
+        functools.partial(final_body, step),
         jax.ShapeDtypeStruct((tokens, model), bf16),
-        [VMEM, HBM, HBM, HBM, HBM, HBM],
+        [VMEM, HBM, HBM, HBM],
         HBM,
         [
-            pltpu.VMEM((model, tokens), f32),
-            pltpu.VMEM((tokens, model), bf16),
-            pltpu.VMEM(output_weight.shape, bf16),
+            pltpu.VMEM((2 * model + tokens, model), bf16),
             pltpu.VMEM(up_weight.shape, bf16),
             pltpu.VMEM(down_weight.shape, bf16),
             pltpu.VMEM((tokens, model), bf16),
-            pltpu.SemaphoreType.DMA((7,)),
+            pltpu.SemaphoreType.DMA((5 + 2 * hidden_chunks,)),
         ],
         flops=2 * tokens * model * 4096,
         name="final",
-        size=60,
-    )(returned.reshape(model, tokens), gates, embedded, output_weight, up_weight, down_weight)
+        size=52,
+    )(returned.reshape(model, tokens), carried, up_weight, down_weight)
     return result[None]
 
 

time: 90.9 us -> 82.6 us (0.909); the launches traced: 89.2 us -> 82.2 us
  Pallas kernels: 58.8 us -> 51.6 us
  waiting for transfers between devices: 11.6 us -> 14.7 us
  starting transfers between devices: 16.3 us -> 14.5 us
  local copies, waits for them, and re-layouts: 2.26 us -> 1.15 us
    pallas_call x1, Pallas kernels: 19.5 us -> 15.8 us  [local(): call(functools.partial(attend_body, groups, seq, cap, hot, width, BQ, BK,...]
    pallas_call x2, Pallas kernels: 14.7 us -> 12.3 us  [the longest x1 6.2 us: local(): call(functools.partial(final_body, step), jax.ShapeDtypeStruct((tokens, m...]
    all_to_all x1, starting transfers between devices: 5.33 us -> 3.47 us  [local(): got = lax.all_to_all(sent, both, split_axis=0, concat_axis=0, tiled=True)]
    all_to_all x1, waiting for transfers between devices: 4.3 us -> 6.16 us  [local(): lax.all_to_all(attended, 'seq', split_axis=0, concat_axis=0, tiled=True)]
    pallas_call x1, Pallas kernels: 11.1 us -> 9.76 us  [local(): call(functools.partial(spread_body, step, seq, lines), jax.ShapeDtypeStru...]
    all_to_all x1, waiting for transfers between devices: 5.13 us -> 6.43 us  [local(): got = lax.all_to_all(sent, both, split_axis=0, concat_axis=0, tiled=True)]
    unnamed x6, local copies, waits for them, and re-layouts: 2.26 us -> 1.15 us
  transfers between devices with their start and end apart: 3 -> 3, of which waited for: 3 -> 3; matrix products, arithmetic and copies ran while one was open for 0% -> 0% of each run, Pallas kernels for 28% -> 26%
where the time goes in v1:
time: 82.6 us; the launch traced here: 82.2 us
  Pallas kernels  51.6 us (62%)
  waiting for transfers between devices  14.7 us (18%)
  starting transfers between devices  14.5 us (18%)
  local copies, waits for them, and re-layouts  1.15 us (1%)
    pallas_call x1, Pallas kernels, local(): call(functools.partial(attend_body, groups, seq, cap, hot, width, BQ, BK,...  15.8 us
    pallas_call x1, Pallas kernels, local(): call(functools.partial(spread_body, step, seq, lines), jax.ShapeDtypeStru...  9.76 us
    all_to_all x1, starting transfers between devices, local(): lax.all_to_all(message, both, split_axis=0, concat_axis=0, tiled=True)  7.33 us
    pallas_call x1, Pallas kernels, local(): call(functools.partial(owner_body, groups, emb, seq, cap), jax.ShapeDtype...  6.48 us
    all_to_all x1, waiting for transfers between devices, local(): got = lax.all_to_all(sent, both, split_axis=0, concat_axis=0, tiled=True)  6.43 us
    pallas_call x1, Pallas kernels, local(): call(functools.partial(final_body, step), jax.ShapeDtypeStruct((tokens, m...  6.2 us
    all_to_all x1, waiting for transfers between devices, local(): lax.all_to_all(attended, 'seq', split_axis=0, concat_axis=0, tiled=True)  6.16 us
    pallas_call x1, Pallas kernels, local(): call(functools.partial(own_body, hot, cap, step), jax.ShapeDtypeStruct((2...  6.12 us
  transfers between devices with their start and end apart: 3, of which 3 were waited for; matrix products, arithmetic and copies ran while one was open for 0% of the time, Pallas kernels for 26%

profile of v1, /device:TPU:0, one launch (start us, length us, event | category | flops | bytes accessed | tf_op | source)
XLA Modules:
  0.0 82.2 jit_solution(16219527084106134685)
XLA Ops:
  0.0 1.6 %message.1.after = s32[32,6,128]{2,1,0:T(8,128)} custom-call(s32[1,512]{1,0:T(1,128)} %ids.3, s32[1,512]{1,0:T(1,128)} %segments.1, s32[4,32]{1,0:T(4,128)} %bitcast.8), custom_call_target="tpu_custom_call" | custom-call | tf_op jit(solution)/shard_map/message/pallas_call | solution.py:503
  1.6 7.3 %all-to-all-start = ((s32[32,6,128]{2,1,0:T(8,128)}), s32[32,6,128]{2,1,0:T(8,128)S(1)}, u32[]{:S(2)}, u32[]{:S(2)}) async-start(s32[32,6,128]{2,1,0:T(8,128)} %message.1.after), calls=%async_computation | async-start | bytes 262144 | tf_op jit(solution)/shard_map/all_to_all | solution.py:511
  8.9 5.7 %hot.1.table_hbm.after = bf16[192,4096]{1,0:T(8,128)(2,1)} custom-call(s32[1]{0:T(128)} %bitcast.3.own, s32[32,6,128]{2,1,0:T(8,128)} %message.1.after, bf16[512,2048]{1,0:T(8,128)(2,1)} %weight_hbm.5, bf16[4096,512]{1,0:T(8,128)(2,1)} %table_hbm.3), custom_call_target="tpu_custom_call" | custom-call | flops 1073741824 | tf_op jit(solution)/shard_map/hot/pallas_call | solution.py:515
  14.6 2.1 %all-to-all-done.heard.message_hbm = s32[32,6,128]{2,1,0:T(8,128)S(1)} async-done(((s32[32,6,128]{2,1,0:T(8,128)}), s32[32,6,128]{2,1,0:T(8,128)S(1)}, u32[]{:S(2)}, u32[]{:S(2)}) %all-to-all-start) | async-done | bytes 98336 | tf_op jit(solution)/shard_map/all_to_all | solution.py:511
  16.7 6.5 %owner.1 = bf16[32,64,128]{2,1,0:T(8,128)(2,1)} custom-call(s32[32,6,128]{2,1,0:T(8,128)S(1)} %all-to-all-done.heard.message_hbm, bf16[8192,512]{1,0:T(8,128)(2,1)} %cold.1, bf16[512,2048]{1,0:T(8,128)(2,1)} %weight_hbm.5, bf16[192,4096]{1,0:T(8,128)(2,1)} %hot.1.table_hbm.after), custom_call_target="tpu_custom_call" | custom-call | flops 268435456 | tf_op jit(solution)/shard_map/owner/pallas_call | solution.py:532
  23.2 3.5 %all-to-all-start.1 = ((bf16[32,64,128]{2,1,0:T(8,128)(2,1)}), bf16[32,64,128]{2,1,0:T(8,128)(2,1)S(1)}, u32[]{:S(2)}, u32[]{:S(2)}) async-start(bf16[32,64,128]{2,1,0:T(8,128)(2,1)} %owner.1), calls=%async_computation.1 | async-start | bytes 1048576 | tf_op jit(solution)/shard_map/all_to_all | solution.py:551
  26.7 9.8 %spread.1.table_hbm = bf16[192,4096]{1,0:T(8,128)(2,1)S(1)} custom-call(s32[1]{0:T(128)} %bitcast.member, s32[32,6,128]{2,1,0:T(8,128)S(1)} %all-to-all-done.heard.message_hbm, bf16[192,4096]{1,0:T(8,128)(2,1)} %hot.1.table_hbm.after), custom_call_target="tpu_custom_call" | custom-call | flops 8589934592 | tf_op jit(solution)/shard_map/spread/pallas_call | solution.py:554
  36.4 0.0 copy-start.1
  36.5 0.0 copy-start.2
  36.5 6.4 %all-to-all-done.1.got = bf16[32,64,128]{2,1,0:T(8,128)(2,1)S(1)} async-done(((bf16[32,64,128]{2,1,0:T(8,128)(2,1)}), bf16[32,64,128]{2,1,0:T(8,128)(2,1)S(1)}, u32[]{:S(2)}, u32[]{:S(2)}) %all-to-all-start.1) | async-done | bytes 524320 | tf_op jit(solution)/shard_map/all_to_all | solution.py:551
  42.9 15.8 %attend.1 = bf16[8,64,512]{2,1,0:T(8,128)(2,1)} custom-call(s32[1]{0:T(128)} %bitcast.member, s32[32,6,128]{2,1,0:T(8,128)S(1)} %all-to-all-done.heard.message_hbm, bf16[192,4096]{1,0:T(8,128)(2,1)S(1)} %spread.1.table_hbm, bf16[32,64,128]{2,1,0:T(8,128)(2,1)S(1)} %all-to-all-done.1.got), custom_call_target="tpu_custom_call" | custom-call | flops 10000000000 | tf_op jit(solution)/shard_map/attend/pallas_call | solution.py:572
  58.7 3.7 %all-to-all-start.2 = ((bf16[8,64,512]{2,1,0:T(8,128)(2,1)}), bf16[8,64,512]{2,1,0:T(8,128)(2,1)S(1)}, u32[]{:S(2)}, u32[]{:S(2)}) async-start(bf16[8,64,512]{2,1,0:T(8,128)(2,1)} %attend.1), calls=%async_computation.2 | async-start | bytes 1048576 | tf_op jit(solution)/shard_map/all_to_all | solution.py:595
  62.4 0.0 copy-done.1
  62.4 0.0 copy-done.2
  62.4 6.1 %own.1.carried_hbm = bf16[1536,512]{1,0:T(8,128)(2,1)S(1)} custom-call(s32[1,512]{1,0:T(1,128)S(1)} %copy-done.2, bf16[32,64,128]{2,1,0:T(8,128)(2,1)S(1)} %all-to-all-done.1.got, bf16[4096,512]{1,0:T(8,128)(2,1)} %table_hbm.3, bf16[512,2048]{1,0:T(8,128)(2,1)} %weight_hbm.5, bf16[512,512]{1,0:T(8,128)(2,1)S(1)} %copy-done.1), custom_call_target="tpu_custom_call" | custom-call | flops 268435456 | tf_op jit(solution)/shard_map/own/pallas_call | solution.py:597
  68.6 0.0 copy-start
  68.6 1.1 %copy-done = bf16[1536,512]{1,0:T(8,128)(2,1)} copy-done((bf16[1536,512]{1,0:T(8,128)(2,1)}, bf16[1536,512]{1,0:T(8,128)(2,1)S(1)}, u32[]{:S(2)}) %copy-start) | copy-done | bytes 1572888
  69.7 6.2 %all-to-all-done.2 = bf16[8,64,512]{2,1,0:T(8,128)(2,1)S(1)} async-done(((bf16[8,64,512]{2,1,0:T(8,128)(2,1)}), bf16[8,64,512]{2,1,0:T(8,128)(2,1)S(1)}, u32[]{:S(2)}, u32[]{:S(2)}) %all-to-all-start.2) | async-done | bytes 524320 | tf_op jit(solution)/shard_map/all_to_all | solution.py:595
  75.9 6.2 %final.1 = bf16[512,512]{1,0:T(8,128)(2,1)} custom-call(bf16[512,512]{1,0:T(8,128)(2,1)S(1)} %bitcast.7, bf16[1536,512]{1,0:T(8,128)(2,1)} %copy-done, bf16[512,2048]{1,0:T(8,128)(2,1)} %up_hbm.1, bf16[2048,512]{1,0:T(8,128)(2,1)} %down_hbm.1), custom_call_target="tpu_custom_call" | custom-call | flops 2147483648 | tf_op jit(solution)/shard_map/final/pallas_call | solution.py:615
Async XLA Ops:
  1.6 15.1 %all-to-all-start = ((s32[32,6,128]{2,1,0:T(8,128)}), s32[32,6,128]{2,1,0:T(8,128)S(1)}, u32[]{:S(2)}, u32[]{:S(2)}) async-start(s32[32,6,128]{2,1,0:T(8,128)} %message.1.after), calls=%async_computation | async-start | bytes 262144 | tf_op jit(solution)/shard_map/all_to_all | solution.py:511
  23.2 19.7 %all-to-all-start.1 = ((bf16[32,64,128]{2,1,0:T(8,128)(2,1)}), bf16[32,64,128]{2,1,0:T(8,128)(2,1)S(1)}, u32[]{:S(2)}, u32[]{:S(2)}) async-start(bf16[32,64,128]{2,1,0:T(8,128)(2,1)} %owner.1), calls=%async_computation.1 | async-start | bytes 1048576 | tf_op jit(solution)/shard_map/all_to_all | solution.py:551
  36.4 26.0 %copy-start.1 = (bf16[512,512]{1,0:T(8,128)(2,1)S(1)}, bf16[512,512]{1,0:T(8,128)(2,1)}, u32[]{:S(2)}) copy-start(bf16[512,512]{1,0:T(8,128)(2,1)} %out_hbm.1) | copy-start | bytes 1572868
  36.5 26.0 %copy-start.2 = (s32[1,512]{1,0:T(1,128)S(1)}, s32[1,512]{1,0:T(1,128)}, u32[]{:S(2)}) copy-start(s32[1,512]{1,0:T(1,128)} %ids.3) | copy-start | bytes 6148
  58.7 17.2 %all-to-all-start.2 = ((bf16[8,64,512]{2,1,0:T(8,128)(2,1)}), bf16[8,64,512]{2,1,0:T(8,128)(2,1)S(1)}, u32[]{:S(2)}, u32[]{:S(2)}) async-start(bf16[8,64,512]{2,1,0:T(8,128)(2,1)} %attend.1), calls=%async_computation.2 | async-start | bytes 1048576 | tf_op jit(solution)/shard_map/all_to_all | solution.py:595
  68.6 1.1 %copy-start = (bf16[1536,512]{1,0:T(8,128)(2,1)}, bf16[1536,512]{1,0:T(8,128)(2,1)S(1)}, u32[]{:S(2)}) copy-start(bf16[1536,512]{1,0:T(8,128)(2,1)S(1)} %own.1.carried_hbm) | copy-start | bytes 4718596
